TPU v7x, 256 devices: a whole 4x4x8 slice. The times are simulated.
256 devices in a mesh: lat: 16 (over z, core), lon: 16 (over y, x).
Axes of the slice: x: 4, y: 4, z: 8, core: 2. Of those that a mesh axis runs over, the one named last changes fastest.
Arguments:
- predicted_state: float32 [1440, 26624], P('lon', 'lat'), may hold values from -24 to 24
- verified_state: float32 [1440, 26624], P('lon', 'lat'), may hold values from -20 to 20
- normal_state: float32 [1440, 26624], P('lon', 'lat'), may hold values from -3 to 3
Outputs:
- energy_curves: float32 [3, 52, 721], replicated
- rms_error: float32 [52], replicated
- anomaly_corr: float32 [52], replicated
All inputs are finite; a program needn't handle non-finite values.
Results may differ from a plain program's by a relative error of at most 0.00005.
Values sent between devices are 32-bit elements; how exact they have to be, the bound alone decides.
No kernel may reach another device: no remote copies, remote signals or barrier semaphores. Data moves between devices by JAX's collectives and lax.ppermute only.
A program may use at most 64 MiB of HBM per device.

v0:
```python
import jax
import jax.numpy as jnp
from jax import lax
from jax.sharding import Mesh
from jax.sharding import PartitionSpec as P

FIELDS = 52
LAT = ("lat_0", "lat_1")
LON = ("lon_0", "lon_1")
LAT_LON = ("lat_0", "lat_1", "lon_0", "lon_1")
epsilon = 1e-06


def gathered_total(value, axis):
    tiles = lax.all_gather(value, axis)
    return tiles.sum(axis=0)


def copy_for_each(value, axis):
    copies = jnp.broadcast_to(value, (lax.axis_size(axis), *value.shape))
    return lax.all_to_all(copies, axis, split_axis=0, concat_axis=0, tiled=True)


def in_order(tiles, dim):
    lengths = list(tiles.shape[1:])
    lengths[dim] *= tiles.shape[0]
    return jnp.moveaxis(tiles, 0, dim).reshape(lengths)


def gather_directly(value, axis, dim):
    tiles = copy_for_each(value, axis)
    return in_order(tiles, dim)


def one_axis_at_a_time(value, axes):
    for axis in axes:
        value = lax.psum(value, axis)
    return value


def latitude_weights(lat_index, parallel_number):
    return jnp.cos(jnp.pi * ((lat_index.astype(jnp.float32) + 0.5) / parallel_number - 0.5))


def dft_table(lon_rows, lon_total, wave_count):
    longitudes = jnp.arange(lon_rows, dtype=jnp.int32)
    waves = jnp.arange(wave_count, dtype=jnp.int32)
    phase = longitudes[:, None] * waves[None, :] % lon_total
    angle = 2.0 * jnp.pi / lon_total * phase.astype(jnp.float32)
    return jnp.concatenate([jnp.cos(angle), -jnp.sin(angle)], axis=1)


def transform_columns(stacked, table):
    return lax.dot_general(
        stacked,
        table,
        (((0,), (0,)), ((), ())),
        precision=lax.Precision.HIGHEST,
        preferred_element_type=jnp.float32,
    )


def row_powers(fore_coeffs, true_coeffs, wave_count):
    diff_coeffs = fore_coeffs - true_coeffs

    def square(coeffs):
        return (
            coeffs[:, :wave_count] * coeffs[:, :wave_count]
            + coeffs[:, wave_count:] * coeffs[:, wave_count:]
        )

    return jnp.stack([square(fore_coeffs), square(true_coeffs), square(diff_coeffs)], axis=1)


def local(predicted_state, verified_state, normal_state):
    quantity_labels = FIELDS
    meridian_lines, meridian_number = predicted_state.shape
    parallel_lines = meridian_number // quantity_labels
    parallel_number = parallel_lines * lax.axis_size(LAT)
    lon_devices = lax.axis_size(LON)
    lon_total = meridian_lines * lon_devices
    wave_count = lon_total // 2 + 1
    row_share = meridian_number // lon_devices
    lat_first = lax.axis_index(LAT) * parallel_lines
    weights = latitude_weights(
        lat_first + jnp.arange(parallel_lines, dtype=jnp.int32), parallel_number
    )
    weight_total = jnp.sum(
        latitude_weights(jnp.arange(parallel_number, dtype=jnp.int32), parallel_number)
    )
    predicted_block = predicted_state.reshape(meridian_lines, parallel_lines, quantity_labels)
    observed_block = verified_state.reshape(meridian_lines, parallel_lines, quantity_labels)
    normal_block = normal_state.reshape(meridian_lines, parallel_lines, quantity_labels)
    mismatch_parts = predicted_block - observed_block
    predicted_anomalies = predicted_block - normal_block
    observed_anomalies = observed_block - normal_block
    broad_layout = weights[None, :, None]
    skill_terms = jnp.stack(
        [
            jnp.sum(broad_layout * mismatch_parts * mismatch_parts, axis=(0, 1)),
            jnp.sum(broad_layout * predicted_anomalies * observed_anomalies, axis=(0, 1)),
            jnp.sum(broad_layout * predicted_anomalies * predicted_anomalies, axis=(0, 1)),
            jnp.sum(broad_layout * observed_anomalies * observed_anomalies, axis=(0, 1)),
        ]
    )
    predicted_meridians = predicted_block.transpose(0, 2, 1).reshape(
        meridian_lines, meridian_number
    )
    true_cols = observed_block.transpose(0, 2, 1).reshape(meridian_lines, meridian_number)
    full_table = dft_table(lon_total, lon_total, wave_count)
    fore_blocks = predicted_meridians.reshape(meridian_lines, lon_devices, row_share)
    true_blocks = true_cols.reshape(meridian_lines, lon_devices, row_share)
    fore_part = lax.all_to_all(fore_blocks, LON, split_axis=1, concat_axis=0, tiled=True)[:, 0, :]
    true_part = lax.all_to_all(true_blocks, LON, split_axis=1, concat_axis=0, tiled=True)[:, 0, :]
    items = fore_part.shape[1]
    stacked = jnp.concatenate([fore_part, true_part], axis=1)
    coeffs = transform_columns(stacked, full_table)
    powers = row_powers(coeffs[:items], coeffs[items:], wave_count)
    share_start = lax.axis_index(LON) * row_share
    global_cols = share_start + jnp.arange(row_share, dtype=jnp.int32)
    field_of = global_cols // parallel_lines
    row_weights = latitude_weights(lat_first + global_cols % parallel_lines, parallel_number)
    row_scale = row_weights / (lon_total * lon_total * weight_total)
    weighted = powers.reshape(row_share, 3 * wave_count) * row_scale[:, None]
    field_index = jnp.arange(quantity_labels, dtype=jnp.int32)
    window = min(quantity_labels, row_share // parallel_lines + 2)
    first_field = share_start // parallel_lines
    window_index = jnp.arange(window, dtype=jnp.int32)
    offset = field_of - first_field
    selector = (offset[None, :] == window_index[:, None]).astype(jnp.float32)
    band_sum = jnp.dot(
        selector, weighted, precision=lax.Precision.HIGHEST, preferred_element_type=jnp.float32
    )
    band_sum = gathered_total(band_sum, LAT)
    gathered = gather_directly(band_sum, LON, 0)
    slot_index = jnp.arange(lon_devices * window, dtype=jnp.int32)
    slot_field = slot_index // window * row_share // parallel_lines + slot_index % window
    placer = (slot_field[None, :] == field_index[:, None]).astype(jnp.float32)
    summed = jnp.dot(
        placer, gathered, precision=lax.Precision.HIGHEST, preferred_element_type=jnp.float32
    )
    energy_curves = summed.reshape(quantity_labels, 3, wave_count).transpose(1, 0, 2)
    skill_means = one_axis_at_a_time(skill_terms, LAT_LON) / (lon_total * weight_total)
    rms_error = jnp.sqrt(skill_means[0])
    anomaly_corr = skill_means[1] / jnp.sqrt(
        (skill_means[2] + epsilon) * (skill_means[3] + epsilon)
    )
    return (energy_curves, rms_error, anomaly_corr)


def solution(mesh):
    split = Mesh(mesh.devices.reshape(8, 2, 4, 4), ("lat_0", "lat_1", "lon_0", "lon_1"))
    placed = (P(LON, LAT), P(LON, LAT), P(LON, LAT))
    return jax.shard_map(
        local, mesh=split, in_specs=placed, out_specs=(P(), P(), P()), check_vma=False
    )
```

profile of v0, /device:TPU:32, one launch (start us, length us, event | category | flops | bytes accessed | tf_op | source)
XLA Modules:
  0.0 134.7 jit_solution(8553598475362706822)
XLA Ops:
  0.6 1.4 %copy.28 = f32[90,1664]{0,1:T(8,128)S(1)} copy(f32[90,1664]{1,0:T(8,128)} %param.4) | data formatting | bytes 1198080 | tf_op args[1]
  2.0 0.1 reshape.127
  2.1 0.2 copy.29
  2.3 1.2 copy.30
  3.5 0.0 copy-start
  3.5 7.2 %all-to-all-start.1 = ((f32[90,16,104]{2,0,1:T(8,128)}), f32[90,16,104]{2,0,1:T(8,128)S(1)}, u32[]{:S(2)}, u32[]{:S(2)}) async-start(f32[90,16,104]{2,0,1:T(8,128)} %copy.30), calls=%async_computation.1 | async-start | bytes 1572864 | tf_op jit(solution)/shard_map/all_to_all | solution.py:114
  10.7 1.4 %copy.24 = f32[90,1664]{0,1:T(8,128)S(1)} copy(f32[90,1664]{1,0:T(8,128)} %param.3) | data formatting | bytes 1198080 | tf_op args[0]
  12.1 0.1 reshape.126
  12.1 0.2 copy.25
  12.3 1.3 copy.26
  13.6 0.1 mul.178
  13.7 0.1 mul.179
  13.8 0.6 cosine_reduce_fusion
  15.1 0.1 fusion.39
  15.2 0.0 copy-done
  15.2 1.6 %fusion.17 = (f32[1664]{0:T(1024)S(1)}, f32[1664]{0:T(1024)S(1)}, f32[1664]{0:T(1024)S(1)}, f32[1664]{0:T(1024)S(1)}) fusion(f32[90,1664]{1,0:T(8,128)} %param.3, f32[90,1664]{1,0:T(8,128)S(1)} %copy-done, f32[1664]{0:T(1024)S(1)} %mul.179, f32[90,1664]{1,0:T(8,128)} %param.5), kind=kLoop, calls=%fused_computation.27 | loop fusion | flops 2089984 | bytes 1830400 | tf_op jit(solution)/shard_map/reduce_sum | solution.py:100
  16.8 8.3 %all-to-all-done.1 = f32[90,16,104]{2,0,1:T(8,128)S(1)} async-done(((f32[90,16,104]{2,0,1:T(8,128)}), f32[90,16,104]{2,0,1:T(8,128)S(1)}, u32[]{:S(2)}, u32[]{:S(2)}) %all-to-all-start.1) | async-done | bytes 599072 | tf_op jit(solution)/shard_map/all_to_all | solution.py:114
  25.2 3.6 %all-to-all-start = ((f32[90,16,104]{2,0,1:T(8,128)}), f32[90,16,104]{2,0,1:T(8,128)S(1)}, u32[]{:S(2)}, u32[]{:S(2)}) async-start(f32[90,16,104]{2,0,1:T(8,128)} %copy.26), calls=%async_computation | async-start | bytes 1572864 | tf_op jit(solution)/shard_map/all_to_all | solution.py:113
  28.8 0.1 reduce_sum.94
  28.9 0.1 reduce_sum.91
  29.0 0.1 reduce_sum.88
  29.2 0.1 reduce_sum.68
  30.0 19.7 %sine_negate_fusion = (f32[1440,721]{1,0:T(8,128)}, f32[1440,721]{1,0:T(8,128)}) fusion(), kind=kLoop, calls=%fused_computation.7 | loop fusion | flops 10382400 | bytes 8305920 | tf_op jit(solution)/shard_map/neg | solution.py:50
  49.7 0.1 reshape.136
  49.7 0.3 copy.35
  50.0 0.0 all-to-all-done
  50.0 0.1 reshape.135
  50.0 0.3 copy.34
  50.3 10.6 %fusion = f32[208,1442]{1,0:T(8,128)S(1)} fusion(f32[1440,721]{1,0:T(8,128)} %get-tuple-element.11, f32[1440,721]{1,0:T(8,128)} %get-tuple-element.12, f32[1440,104]{0,1:T(8,128)S(1)} %copy.35, f32[1440,104]{0,1:T(8,128)S(1)} %copy.34), kind=kOutput, calls=%fused_computation | convolution fusion | flops 5185270272 | bytes 10703744 | tf_op jit(solution)/shard_map/dot_general | solution.py:54
  61.0 0.1 slice_subtract_fusion
  61.0 0.2 fusion.25
  61.3 0.2 fusion.21
  61.4 0.1 pad_maximum_fusion
  61.5 0.4 copy.32
  61.9 0.1 reshape.128
  62.0 0.7 convolution_bitcast_fusion
  62.7 21.0 %all-gather.1 = f32[16,5,2163]{2,1,0:T(8,128)S(1)} all-gather(f32[1,5,2163]{2,1,0:T(8,128)S(1)} %convolution_bitcast_fusion), channel_id=2, replica_groups=mesh['lat_0'=8,'lat_1'=2,'lon_0'=4,'lon_1'=4] {'lat_0','lat_1'}, dimensions={0}, use_global_device_ids=true | all-gather | bytes 735420 | tf_op jit(solution)/shard_map/all_gather | solution.py:15
  83.7 0.1 reduce_sum.66
  83.8 1.1 broadcast_in_dim.2
  84.9 7.2 %all-to-all-start.2 = ((f32[16,5,2163]{2,1,0:T(8,128)}), f32[16,5,2163]{2,1,0:T(8,128)S(1)}, u32[]{:S(2)}, u32[]{:S(2)}) async-start(f32[16,5,2163]{2,1,0:T(8,128)} %broadcast_in_dim.2), calls=%async_computation.2 | async-start | bytes 2228224 | tf_op jit(solution)/shard_map/all_to_all | solution.py:21
  92.1 16.3 %psum.28 = f32[4,52]{1,0:T(4,128)S(1)} all-reduce(f32[4,52]{1,0:T(4,128)S(1)} %pad_maximum_fusion.1), channel_id=1, replica_groups=mesh['lat_0'=8,'lat_1'=2,'lon_0'=4,'lon_1'=4] {'lat_0'}, use_global_device_ids=true, to_apply=%region_10.11 | all-reduce | flops 208 | bytes 1664 | tf_op jit(solution)/shard_map/psum | solution.py:37
  108.4 2.5 %psum.29 = f32[4,52]{1,0:T(4,128)S(1)} all-reduce(f32[4,52]{1,0:T(4,128)S(1)} %psum.28), channel_id=1, replica_groups=mesh['lat_0'=8,'lat_1'=2,'lon_0'=4,'lon_1'=4] {'lat_1'}, use_global_device_ids=true, to_apply=%region_11.12 | all-reduce | flops 208 | bytes 1664 | tf_op jit(solution)/shard_map/psum | solution.py:37
  110.8 10.8 %psum.30 = f32[4,52]{1,0:T(4,128)S(1)} all-reduce(f32[4,52]{1,0:T(4,128)S(1)} %psum.29), channel_id=1, replica_groups=mesh['lat_0'=8,'lat_1'=2,'lon_0'=4,'lon_1'=4] {'lon_0'}, use_global_device_ids=true, to_apply=%region_12.13 | all-reduce | flops 208 | bytes 1664 | tf_op jit(solution)/shard_map/psum | solution.py:37
  121.7 10.4 %psum.31 = f32[4,52]{1,0:T(4,128)S(1)} all-reduce(f32[4,52]{1,0:T(4,128)S(1)} %psum.30), channel_id=1, replica_groups=mesh['lat_0'=8,'lat_1'=2,'lon_0'=4,'lon_1'=4] {'lon_1'}, use_global_device_ids=true, to_apply=%region_13.14 | all-reduce | flops 208 | bytes 1664 | tf_op jit(solution)/shard_map/psum | solution.py:37
  132.1 0.5 multiply_bitcast_fusion
  132.6 0.0 all-to-all-done.2
  132.6 0.1 reshape.129
  132.7 0.7 dot_general.16
  133.4 1.3 convolution_bitcast_fusion.1
  (9 shorter events, 0.2 us)
Async XLA Ops:
  3.5 11.7 %copy-start = (f32[90,1664]{1,0:T(8,128)S(1)}, f32[90,1664]{1,0:T(8,128)}, u32[]{:S(2)}) copy-start(f32[90,1664]{1,0:T(8,128)} %param.4) | copy-start | bytes 1797124
  3.5 21.7 %all-to-all-start.1 = ((f32[90,16,104]{2,0,1:T(8,128)}), f32[90,16,104]{2,0,1:T(8,128)S(1)}, u32[]{:S(2)}, u32[]{:S(2)}) async-start(f32[90,16,104]{2,0,1:T(8,128)} %copy.30), calls=%async_computation.1 | async-start | bytes 1572864 | tf_op jit(solution)/shard_map/all_to_all | solution.py:114
  25.2 24.8 %all-to-all-start = ((f32[90,16,104]{2,0,1:T(8,128)}), f32[90,16,104]{2,0,1:T(8,128)S(1)}, u32[]{:S(2)}, u32[]{:S(2)}) async-start(f32[90,16,104]{2,0,1:T(8,128)} %copy.26), calls=%async_computation | async-start | bytes 1572864 | tf_op jit(solution)/shard_map/all_to_all | solution.py:113
  84.9 47.7 %all-to-all-start.2 = ((f32[16,5,2163]{2,1,0:T(8,128)}), f32[16,5,2163]{2,1,0:T(8,128)S(1)}, u32[]{:S(2)}, u32[]{:S(2)}) async-start(f32[16,5,2163]{2,1,0:T(8,128)} %broadcast_in_dim.2), calls=%async_computation.2 | async-start | bytes 2228224 | tf_op jit(solution)/shard_map/all_to_all | solution.py:21
where the time goes:
time: 135 us
  blocking collectives  61 us (45%)
  other arithmetic  23.4 us (17%)
  starting transfers between devices  17.9 us (13%)
  matrix products  12.6 us (9%)
  local copies, waits for them, and re-layouts  9.22 us (7%)
  waiting for transfers between devices  8.32 us (6%)
  between operations  2.19 us (2%)
    psum x4, blocking collectives, one_axis_at_a_time(): value = lax.psum(value, axis)  40 us
    all_gather x1, blocking collectives, gathered_total(): tiles = lax.all_gather(value, axis)  21 us
    neg x1, other arithmetic, dft_table(): return jnp.concatenate([jnp.cos(angle), -jnp.sin(angle)], axis=1)  19.7 us
    dot_general x1, matrix products, transform_columns(): lax.dot_general(stacked, table, (((0,), (0,)), ((), ())), precision=lax.P...  10.6 us
    all_to_all x1, waiting for transfers between devices, local(): lax.all_to_all(true_blocks, LON, split_axis=1, concat_axis=0, tiled=True)  8.32 us
    all_to_all x1, starting transfers between devices, local(): lax.all_to_all(true_blocks, LON, split_axis=1, concat_axis=0, tiled=True)  7.17 us
    all_to_all x1, starting transfers between devices, copy_for_each(): return lax.all_to_all(copies, axis, split_axis=0, concat_axis=0, tiled=True)  7.15 us
    all_to_all x1, starting transfers between devices, local(): lax.all_to_all(fore_blocks, LON, split_axis=1, concat_axis=0, tiled=True)  3.61 us
  transfers between devices with their start and end apart: 3, of which 1 were waited for; matrix products, arithmetic and copies ran while one was open for 20% of the time, Pallas kernels for 0%

commit v1 on v0

--- a/solution.py
+++ b/solution.py
@@ -34,7 +34,7 @@
 
 def one_axis_at_a_time(value, axes):
     for axis in axes:
-        value = lax.psum(value, axis)
+        value = jnp.sum(lax.all_gather(value, axis), axis=0)
     return value
 
 

time: 135 us -> 143 us (1.059); the launches traced: 135 us -> 140 us
  blocking collectives: 61 us -> 66.6 us
    all_gather x0 -> x4, blocking collectives: none -> 45.5 us  [one_axis_at_a_time(): value = jnp.sum(lax.all_gather(value, axis), axis=0)]
    psum x4 -> x0, blocking collectives: 40 us -> none  [one_axis_at_a_time(): value = lax.psum(value, axis)]
  transfers between devices with their start and end apart: 3 -> 3, of which waited for: 1 -> 1; matrix products, arithmetic and copies ran while one was open for 20% -> 19% of each run, Pallas kernels for 0% -> 0%
where the time goes in v1:
time: 143 us; the launch traced here: 140 us
  blocking collectives  66.6 us (47%)
  other arithmetic  23.4 us (16%)
  starting transfers between devices  17.9 us (13%)
  matrix products  12.6 us (9%)
  local copies, waits for them, and re-layouts  9.22 us (6%)
  waiting for transfers between devices  8.32 us (6%)
  between operations  2.19 us (2%)
    all_gather x4, blocking collectives, one_axis_at_a_time(): value = jnp.sum(lax.all_gather(value, axis), axis=0)  45.5 us
    all_gather x1, blocking collectives, gathered_total(): tiles = lax.all_gather(value, axis)  21 us
    neg x1, other arithmetic, dft_table(): return jnp.concatenate([jnp.cos(angle), -jnp.sin(angle)], axis=1)  19.7 us
    dot_general x1, matrix products, transform_columns(): lax.dot_general(stacked, table, (((0,), (0,)), ((), ())), precision=lax.P...  10.6 us
    all_to_all x1, waiting for transfers between devices, local(): lax.all_to_all(true_blocks, LON, split_axis=1, concat_axis=0, tiled=True)  8.32 us
    all_to_all x1, starting transfers between devices, local(): lax.all_to_all(true_blocks, LON, split_axis=1, concat_axis=0, tiled=True)  7.17 us
    all_to_all x1, starting transfers between devices, copy_for_each(): return lax.all_to_all(copies, axis, split_axis=0, concat_axis=0, tiled=True)  7.15 us
    all_to_all x1, starting transfers between devices, local(): lax.all_to_all(fore_blocks, LON, split_axis=1, concat_axis=0, tiled=True)  3.61 us
  transfers between devices with their start and end apart: 3, of which 1 were waited for; matrix products, arithmetic and copies ran while one was open for 19% of the time, Pallas kernels for 0%

profile of v1, /device:TPU:32, one launch (start us, length us, event | category | flops | bytes accessed | tf_op | source)
XLA Modules:
  0.0 140.3 jit_solution(6316962664088923390)
XLA Ops:
  0.6 1.4 copy.28
  2.0 0.1 reshape.127
  2.1 0.2 copy.29
  2.3 1.2 copy.30
  3.5 0.0 copy-start
  3.5 7.2 %all-to-all-start.1 = ((f32[90,16,104]{2,0,1:T(8,128)}), f32[90,16,104]{2,0,1:T(8,128)S(1)}, u32[]{:S(2)}, u32[]{:S(2)}) async-start(f32[90,16,104]{2,0,1:T(8,128)} %copy.30), calls=%async_computation.1 | async-start | bytes 1572864 | tf_op jit(solution)/shard_map/all_to_all | solution.py:114
  10.7 1.4 copy.24
  12.1 0.1 reshape.126
  12.1 0.2 copy.25
  12.3 1.3 copy.26
  13.6 0.1 mul.178
  13.7 0.1 mul.179
  13.8 0.6 cosine_reduce_fusion
  15.1 0.1 fusion.39
  15.2 0.0 copy-done
  15.2 1.6 %fusion.17 = (f32[1664]{0:T(1024)S(1)}, f32[1664]{0:T(1024)S(1)}, f32[1664]{0:T(1024)S(1)}, f32[1664]{0:T(1024)S(1)}) fusion(f32[90,1664]{1,0:T(8,128)} %param.3, f32[90,1664]{1,0:T(8,128)S(1)} %copy-done, f32[1664]{0:T(1024)S(1)} %mul.179, f32[90,1664]{1,0:T(8,128)} %param.5), kind=kLoop, calls=%fused_computation.27 | loop fusion | flops 2089984 | bytes 1830400 | tf_op jit(solution)/shard_map/reduce_sum | solution.py:100
  16.8 8.3 %all-to-all-done.1 = f32[90,16,104]{2,0,1:T(8,128)S(1)} async-done(((f32[90,16,104]{2,0,1:T(8,128)}), f32[90,16,104]{2,0,1:T(8,128)S(1)}, u32[]{:S(2)}, u32[]{:S(2)}) %all-to-all-start.1) | async-done | bytes 599072 | tf_op jit(solution)/shard_map/all_to_all | solution.py:114
  25.2 3.6 %all-to-all-start = ((f32[90,16,104]{2,0,1:T(8,128)}), f32[90,16,104]{2,0,1:T(8,128)S(1)}, u32[]{:S(2)}, u32[]{:S(2)}) async-start(f32[90,16,104]{2,0,1:T(8,128)} %copy.26), calls=%async_computation | async-start | bytes 1572864 | tf_op jit(solution)/shard_map/all_to_all | solution.py:113
  28.8 0.1 reduce_sum.130
  28.9 0.1 reduce_sum.127
  29.0 0.1 reduce_sum.124
  29.2 0.1 reduce_sum.121
  29.3 19.7 %sine_negate_fusion = (f32[1440,721]{1,0:T(8,128)}, f32[1440,721]{1,0:T(8,128)}) fusion(), kind=kLoop, calls=%fused_computation.7 | loop fusion | flops 10382400 | bytes 8305920 | tf_op jit(solution)/shard_map/neg | solution.py:50
  49.0 0.1 reshape.152
  49.1 0.3 copy.35
  49.3 0.0 all-to-all-done
  49.3 0.1 reshape.151
  49.4 0.3 copy.34
  49.7 10.6 %fusion = f32[208,1442]{1,0:T(8,128)S(1)} fusion(f32[1440,721]{1,0:T(8,128)} %get-tuple-element.11, f32[1440,721]{1,0:T(8,128)} %get-tuple-element.12, f32[1440,104]{0,1:T(8,128)S(1)} %copy.35, f32[1440,104]{0,1:T(8,128)S(1)} %copy.34), kind=kOutput, calls=%fused_computation | convolution fusion | flops 5185270272 | bytes 10703744 | tf_op jit(solution)/shard_map/dot_general | solution.py:54
  60.3 0.1 slice_subtract_fusion
  60.4 0.2 fusion.25
  60.6 0.2 fusion.21
  60.8 0.1 pad_maximum_fusion
  60.9 0.4 copy.32
  61.3 0.1 reshape.128
  61.3 0.7 convolution_bitcast_fusion
  62.0 21.0 %all-gather.5 = f32[16,5,2163]{2,1,0:T(8,128)S(1)} all-gather(f32[1,5,2163]{2,1,0:T(8,128)S(1)} %convolution_bitcast_fusion), channel_id=2, replica_groups=mesh['lat_0'=8,'lat_1'=2,'lon_0'=4,'lon_1'=4] {'lat_0','lat_1'}, dimensions={0}, use_global_device_ids=true | all-gather | bytes 735420 | tf_op jit(solution)/shard_map/all_gather | solution.py:15
  83.1 0.1 reduce_sum.101
  83.2 1.1 broadcast_in_dim.2
  84.2 7.2 %all-to-all-start.2 = ((f32[16,5,2163]{2,1,0:T(8,128)}), f32[16,5,2163]{2,1,0:T(8,128)S(1)}, u32[]{:S(2)}, u32[]{:S(2)}) async-start(f32[16,5,2163]{2,1,0:T(8,128)} %broadcast_in_dim.2), calls=%async_computation.2 | async-start | bytes 2228224 | tf_op jit(solution)/shard_map/all_to_all | solution.py:21
  91.4 21.0 %all-gather.6 = f32[8,4,52]{2,1,0:T(4,128)S(1)} all-gather(f32[1,4,52]{2,1,0:T(4,128)S(1)} %maximum_bitcast_fusion), channel_id=3, replica_groups=mesh['lat_0'=8,'lat_1'=2,'lon_0'=4,'lon_1'=4] {'lat_0'}, dimensions={0}, use_global_device_ids=true | all-gather | bytes 7488 | tf_op jit(solution)/shard_map/all_gather | solution.py:37
  112.5 1.8 %all-gather.7 = f32[2,4,52]{2,1,0:T(4,128)S(1)} all-gather(f32[1,4,52]{2,1,0:T(4,128)S(1)} %bitcast.56), channel_id=4, replica_groups=mesh['lat_0'=8,'lat_1'=2,'lon_0'=4,'lon_1'=4] {'lat_1'}, dimensions={0}, use_global_device_ids=true | all-gather | bytes 2496 | tf_op jit(solution)/shard_map/all_gather | solution.py:37
  114.3 11.6 %all-gather.8 = f32[4,4,52]{2,1,0:T(4,128)S(1)} all-gather(f32[1,4,52]{2,1,0:T(4,128)S(1)} %bitcast.57), channel_id=5, replica_groups=mesh['lat_0'=8,'lat_1'=2,'lon_0'=4,'lon_1'=4] {'lon_0'}, dimensions={0}, use_global_device_ids=true | all-gather | bytes 4160 | tf_op jit(solution)/shard_map/all_gather | solution.py:37
  125.9 11.1 %all-gather.9 = f32[4,4,52]{2,1,0:T(4,128)S(1)} all-gather(f32[1,4,52]{2,1,0:T(4,128)S(1)} %bitcast.58), channel_id=6, replica_groups=mesh['lat_0'=8,'lat_1'=2,'lon_0'=4,'lon_1'=4] {'lon_1'}, dimensions={0}, use_global_device_ids=true | all-gather | bytes 4160 | tf_op jit(solution)/shard_map/all_gather | solution.py:37
  137.7 0.5 multiply_bitcast_fusion
  138.2 0.0 all-to-all-done.2
  138.2 0.1 reshape.129
  138.3 0.7 dot_general.16
  139.0 1.3 convolution_bitcast_fusion.1
  (13 shorter events, 0.3 us)
Async XLA Ops:
  3.5 11.7 %copy-start = (f32[90,1664]{1,0:T(8,128)S(1)}, f32[90,1664]{1,0:T(8,128)}, u32[]{:S(2)}) copy-start(f32[90,1664]{1,0:T(8,128)} %param.4) | copy-start | bytes 1797124
  3.5 21.7 %all-to-all-start.1 = ((f32[90,16,104]{2,0,1:T(8,128)}), f32[90,16,104]{2,0,1:T(8,128)S(1)}, u32[]{:S(2)}, u32[]{:S(2)}) async-start(f32[90,16,104]{2,0,1:T(8,128)} %copy.30), calls=%async_computation.1 | async-start | bytes 1572864 | tf_op jit(solution)/shard_map/all_to_all | solution.py:114
  25.2 24.2 %all-to-all-start = ((f32[90,16,104]{2,0,1:T(8,128)}), f32[90,16,104]{2,0,1:T(8,128)S(1)}, u32[]{:S(2)}, u32[]{:S(2)}) async-start(f32[90,16,104]{2,0,1:T(8,128)} %copy.26), calls=%async_computation | async-start | bytes 1572864 | tf_op jit(solution)/shard_map/all_to_all | solution.py:113
  84.2 54.0 %all-to-all-start.2 = ((f32[16,5,2163]{2,1,0:T(8,128)}), f32[16,5,2163]{2,1,0:T(8,128)S(1)}, u32[]{:S(2)}, u32[]{:S(2)}) async-start(f32[16,5,2163]{2,1,0:T(8,128)} %broadcast_in_dim.2), calls=%async_computation.2 | async-start | bytes 2228224 | tf_op jit(solution)/shard_map/all_to_all | solution.py:21
